TPU v7x, 32 devices: a whole 2x2x4 slice. The times are simulated.
32 devices in a mesh: beam: 8 (over z, y), mp: 4 (over x, core).
Axes of the slice: x: 2, y: 2, z: 4, core: 2. Of those that a mesh axis runs over, the one named last changes fastest.
Arguments:
- token_ids: int32 [512], P('beam'), may hold values from 0 to 128255
- parents: int32 [64, 8, 1], P('beam'), may hold values from 0 to 7; in each aligned block of 512 rows (0 to 511, 512 to 1023, ..., all dimensions but the last counted through in order) at most 192 rows name the same one
- embedding: bfloat16 [128256, 8192], P('mp', 'beam'), may hold values from -6 to 6
- norm_gain: bfloat16 [8192], P('beam'), may hold values from 0.099609375 to 1.8984375
- query_weight: bfloat16 [8192, 8192], P('beam', 'mp'), may hold values from -0.0625 to 0.0625
- key_weight: bfloat16 [8192, 1024], P('beam', 'mp'), may hold values from -0.0625 to 0.0625
- value_weight: bfloat16 [8192, 1024], P('beam', 'mp'), may hold values from -0.0625 to 0.0625
- output_weight: bfloat16 [8192, 8192], P('mp', 'beam'), may hold values from -0.0625 to 0.0625
- cache_keys: bfloat16 [512, 512, 1024], P('beam', None, 'mp'), may hold values from -30 to 30
- cache_values: bfloat16 [512, 512, 1024], P('beam', None, 'mp'), may hold values from -32 to 32
Outputs:
- attention_out: bfloat16 [512, 8192], P('mp', 'beam')
- new_keys: bfloat16 [512, 1024], P('beam', 'mp')
- new_values: bfloat16 [512, 1024], P('beam', 'mp')
Inputs may be any that keep to these rules, and one draw needn't show every extreme that they name: parents lie in 0 to 7. Split the requests into aligned blocks of 64 requests; among the new beams of one block, no parent index is named more than 192 times, and in some blocks one is named exactly 192 times.
All inputs are finite; a program needn't handle non-finite values.
Results may differ from a plain program's by a relative error of at most 0.0071.
The roundings to bfloat16 on the way count: a program that leaves them out, or rounds other values in their place, can miss the bound.
Values may be sent and summed in bfloat16 or wider, within the bound.
No kernel may reach another device: no remote copies, remote signals or barrier semaphores. Data moves between devices by JAX's collectives and lax.ppermute only.
A program may use at most 320 MiB of HBM per device.

v0:
```python
import jax
import jax.numpy as jnp
from jax import lax
from jax.sharding import PartitionSpec as P

D = 8192
HEAD_DIM = 128
LEN = 512
REQS = 64
BEAMS = 8
LOAD = 3
epsilon = 1e-05
rope_base = 500000.0


def apply_rotary(tensor):
    half_dim = HEAD_DIM // 2
    frequency = rope_base ** (-(jnp.arange(half_dim, dtype=jnp.float32) * 2.0 / HEAD_DIM))
    angles = LEN * frequency
    cosine_table = jnp.cos(angles)
    sine_part = jnp.sin(angles)
    front_half = tensor[..., :half_dim]
    back_half = tensor[..., half_dim:]
    return jnp.concatenate(
        [
            front_half * cosine_table - back_half * sine_part,
            back_half * cosine_table + front_half * sine_part,
        ],
        axis=-1,
    )


def finish(query_total, key_total, value_total, square_total):
    inverse = (1.0 / jnp.sqrt(square_total / D + epsilon))[:, None]
    row_count = query_total.shape[0]
    query_matrix = (
        apply_rotary((query_total * inverse).reshape(row_count, -1, HEAD_DIM))
        .astype(jnp.bfloat16)
        .reshape(row_count, -1)
    )
    fresh_keys = (
        apply_rotary((key_total * inverse).reshape(row_count, -1, HEAD_DIM))
        .astype(jnp.bfloat16)
        .reshape(row_count, -1)
    )
    fresh_values = (value_total * inverse).astype(jnp.bfloat16)
    return (query_matrix, fresh_keys, fresh_values)


def attend(query_matrix, self_key_rows, own_values, slot_keys, slot_values):
    scale_factor = HEAD_DIM ** (-0.5)
    scores = (
        jnp.einsum("bkgd,blkd->bkgl", query_matrix, slot_keys, preferred_element_type=jnp.float32)
        * scale_factor
    )
    own_score = (
        jnp.einsum("nlem,nlm->nle", query_matrix, self_key_rows, preferred_element_type=jnp.float32)
        * scale_factor
    )
    ceiling = jnp.maximum(jnp.max(scores, axis=-1), own_score)
    weights = jnp.exp(scores - ceiling[..., None])
    own_weight = jnp.exp(own_score - ceiling)
    softmax_divisor = jnp.sum(weights, axis=-1) + own_weight
    attention_weights = (weights / softmax_divisor[..., None]).astype(jnp.bfloat16)
    own_share = (own_weight / softmax_divisor).astype(jnp.bfloat16)
    mixture = jnp.einsum(
        "bkgl,blkd->bkgd", attention_weights, slot_values, preferred_element_type=jnp.float32
    )
    mixture = (
        mixture
        + own_share.astype(jnp.float32)[..., None] * own_values.astype(jnp.float32)[:, :, None, :]
    )
    return mixture.astype(jnp.bfloat16)


def body(
    token_ids,
    parents,
    embedding,
    norm_gain,
    query_weight,
    key_weight,
    value_weight,
    output_weight,
    cache_keys,
    cache_values,
):
    all_ids, all_parents = (
        lax.all_gather(token_ids, "beam", axis=0, tiled=True),
        lax.all_gather(parents, "beam", axis=0, tiled=True),
    )
    vocab_local = embedding.shape[0]
    vocab_start = lax.axis_index("mp") * vocab_local
    one_hot = (
        all_ids[:, None] == vocab_start + lax.broadcasted_iota(jnp.int32, (1, vocab_local), 1)
    ).astype(jnp.bfloat16)
    looked_up = jnp.dot(one_hot, embedding, preferred_element_type=jnp.float32)
    embedded = lax.psum(looked_up.astype(jnp.bfloat16), "mp")
    widened = embedded.astype(jnp.float32)
    squares = jnp.sum(widened * widened, axis=1)
    scaled = (widened * norm_gain.astype(jnp.float32)[None, :]).astype(jnp.bfloat16)
    query_portion = jnp.dot(scaled, query_weight, preferred_element_type=jnp.float32)
    key_part = jnp.dot(scaled, key_weight, preferred_element_type=jnp.float32)
    value_part = jnp.dot(scaled, value_weight, preferred_element_type=jnp.float32)
    row_local = cache_keys.shape[0]
    first_row = lax.axis_index("beam") * row_local
    query_total, key_total, value_total, square_total = lax.psum(
        (query_portion, key_part, value_part, squares), "beam"
    )
    query_matrix, fresh_keys, fresh_values = finish(
        query_total, key_total, value_total, square_total
    )
    keys_out = lax.dynamic_slice_in_dim(fresh_keys, first_row, row_local, 0)
    values_out = lax.dynamic_slice_in_dim(fresh_values, first_row, row_local, 0)
    key_heads = key_weight.shape[1] // HEAD_DIM
    query_heads = query_weight.shape[1] // HEAD_DIM
    groups = query_heads // key_heads
    query_width = query_heads * HEAD_DIM
    key_width = key_heads * HEAD_DIM
    parent_beam = first_row // REQS
    request_start = first_row % REQS
    offspring_query_rows = lax.dynamic_slice_in_dim(
        query_matrix.reshape(BEAMS, REQS, query_width), request_start, row_local, 1
    )
    child_keys = lax.dynamic_slice_in_dim(
        fresh_keys.reshape(BEAMS, REQS, key_width), request_start, row_local, 1
    )
    child_values = lax.dynamic_slice_in_dim(
        fresh_values.reshape(BEAMS, REQS, key_width), request_start, row_local, 1
    )
    parent_block = lax.dynamic_slice_in_dim(all_parents[:, :, 0], request_start, row_local, 0)
    matches = jnp.transpose(parent_block) == parent_beam
    slot_keys = cache_keys.reshape(row_local, LEN, key_heads, HEAD_DIM)
    slot_values = cache_values.reshape(row_local, LEN, key_heads, HEAD_DIM)
    count_all = BEAMS * row_local
    is_child = matches.reshape(count_all).astype(jnp.int32)
    position = jnp.cumsum(is_child) - 1
    capacity = LOAD * row_local
    select_ones = (
        (position[None, :] == lax.broadcasted_iota(jnp.int32, (capacity, 1), 0))
        & (is_child[None, :] == 1)
    ).astype(jnp.int32)
    selector = select_ones.astype(jnp.bfloat16)
    slot_index = jnp.sum(
        select_ones * (lax.broadcasted_iota(jnp.int32, (1, count_all), 1) % row_local), axis=1
    )
    packed = jnp.concatenate(
        [
            offspring_query_rows.reshape(count_all, query_width),
            child_keys.reshape(count_all, key_width),
            child_values.reshape(count_all, key_width),
        ],
        axis=1,
    )
    picked = jnp.dot(selector, packed, preferred_element_type=jnp.float32).astype(jnp.bfloat16)
    mixture = attend(
        picked[:, :query_width].reshape(capacity, key_heads, groups, HEAD_DIM),
        picked[:, query_width : query_width + key_width].reshape(capacity, key_heads, HEAD_DIM),
        picked[:, query_width + key_width :].reshape(capacity, key_heads, HEAD_DIM),
        slot_keys[slot_index],
        slot_values[slot_index],
    )
    masked_rows = (
        jnp.dot(
            jnp.transpose(selector),
            mixture.reshape(capacity, query_width),
            preferred_element_type=jnp.float32,
        )
        .astype(jnp.bfloat16)
        .reshape(BEAMS, row_local, query_width)
    )
    positioned_rows = lax.dynamic_update_slice_in_dim(
        jnp.zeros((BEAMS, REQS, query_width), jnp.float32),
        masked_rows.astype(jnp.float32),
        request_start,
        1,
    )
    attended = lax.psum(
        positioned_rows.reshape(BEAMS * REQS, query_width).astype(jnp.bfloat16), "beam"
    )
    attention_out = lax.psum_scatter(
        jnp.dot(attended, output_weight, preferred_element_type=jnp.float32),
        "mp",
        scatter_dimension=0,
        tiled=True,
    ).astype(jnp.bfloat16)
    return (attention_out, keys_out, values_out)


def solution(mesh):
    return jax.shard_map(
        body,
        mesh=mesh,
        in_specs=(
            P("beam"),
            P("beam", None, None),
            P("mp", "beam"),
            P("beam"),
            P("beam", "mp"),
            P("beam", "mp"),
            P("beam", "mp"),
            P("mp", "beam"),
            P("beam", None, "mp"),
            P("beam", None, "mp"),
        ),
        out_specs=(P("mp", "beam"), P("beam", "mp"), P("beam", "mp")),
        check_vma=False,
    )
```

profile of v0, /device:TPU:0, one launch (start us, length us, event | category | flops | bytes accessed | tf_op | source)
XLA Modules:
  0.0 505.2 jit_solution(15561030509055637348)
XLA Ops:
  7.3 1.3 dynamic-slice
  9.2 0.9 dynamic-update-slice
  10.1 13.1 %all-reduce = s32[512]{0:T(512)S(1)} all-reduce(s32[512]{0:T(512)S(1)} %dynamic-update-slice), channel_id=1, replica_groups=mesh['beam'=8,'mp'=4] {'beam'}, use_global_device_ids=true, to_apply=%add | all-reduce | flops 512 | bytes 4096
  23.2 40.7 %fusion.16 = bf16[512,1024]{1,0:T(8,128)(2,1)} fusion(bf16[32064,1024]{1,0:T(8,128)(2,1)} %param.12, s32[32064]{0:T(1024)S(1)} %iota_add_fusion, s32[512]{0:T(512)S(1)} %all-reduce), kind=kOutput, calls=%fused_computation.31 | convolution fusion | flops 33638481920 | bytes 66845952 | tf_op jit(solution)/shard_map/dot_general | solution.py:97
  64.0 34.6 %all-reduce.6.cloned.1.call-done = bf16[512,1024]{1,0:T(8,128)(2,1)} async-done(((bf16[512,1024]{1,0:T(8,128)(2,1)}), bf16[512,1024]{1,0:T(8,128)(2,1)}) %all-reduce.6.cloned.1.call-update) | async-done | bytes 1048592 | tf_op jit(solution)/shard_map/psum | solution.py:98
  98.6 6.9 %fusion.23 = f32[512,2048]{1,0:T(8,128)} fusion(bf16[1024,2048]{1,0:T(8,128)(2,1)} %param.14, bf16[512,1024]{1,0:T(8,128)(2,1)} %all-reduce.6.cloned.1.call-done, f32[1024]{0:T(1024)S(1)} %convert_element_type.98), kind=kOutput, calls=%fused_computation.34 | convolution fusion | flops 2149056512 | bytes 9441280 | tf_op jit(solution)/shard_map/dot_general | solution.py:102
  105.5 1.2 fusion.19
  106.7 1.3 fusion.21
  108.1 31.9 %all_gather.6 = s32[64,8,1]{1,2,0:T(1,128)S(1)} all-gather(s32[8,8,1]{1,2,0:T(1,128)S(1)} %copy-done.3), channel_id=1, replica_groups=mesh['beam'=8,'mp'=4] {'beam'}, dimensions={0}, use_global_device_ids=true | all-gather | bytes 2304 | tf_op jit(solution)/shard_map/all_gather | solution.py:90
  140.1 0.3 reduce-window.9
  140.7 22.5 %copy.43 = bf16[64,512,256]{1,2,0:T(8,128)(2,1)} copy(bf16[64,512,256]{2,1,0:T(8,128)(2,1)} %param.18) | data formatting | bytes 33554432 | tf_op args[8]
  163.2 22.2 %copy.44 = bf16[64,512,2,128]{3,1,2,0:T(8,128)(2,1)} copy(bf16[64,512,2,128]{1,3,2,0:T(8,128)(2,1)} %bitcast.61) | data formatting | bytes 33554432 | tf_op jit(solution)/shard_map/reshape | solution.py:133
  185.4 22.5 %copy.49 = bf16[64,512,256]{1,2,0:T(8,128)(2,1)} copy(bf16[64,512,256]{2,1,0:T(8,128)(2,1)} %param.19) | data formatting | bytes 33554432 | tf_op args[9]
  208.0 22.4 %copy.50 = bf16[64,512,2,128]{3,1,2,0:T(8,128)(2,1)} copy(bf16[64,512,2,128]{1,3,2,0:T(8,128)(2,1)} %bitcast.62) | data formatting | bytes 33554432 | tf_op jit(solution)/shard_map/reshape | solution.py:134
  230.4 0.1 slice_reduce_fusion
  230.6 0.2 select_reduce_fusion
  230.8 25.1 %gather_fusion = bf16[192,512,2,128]{3,1,2,0:T(8,128)(2,1)} fusion(bf16[64,512,2,128]{3,1,2,0:T(8,128)(2,1)} %copy.44, s32[1024]{0:T(1024)S(1)} %pad_clamp_fusion), kind=kCustom, calls=%fused_computation | custom fusion | bytes 100664064 | tf_op jit(solution)/shard_map/gather | solution.py:160
  255.9 23.7 %gather_fusion.1 = bf16[192,512,2,128]{3,1,2,0:T(8,128)(2,1)} fusion(bf16[64,512,2,128]{3,1,2,0:T(8,128)(2,1)} %copy.50, s32[1024]{0:T(1024)S(1)} %pad_clamp_fusion), kind=kCustom, calls=%fused_computation.1 | custom fusion | bytes 100664064 | tf_op jit(solution)/shard_map/gather | solution.py:161
  279.7 0.3 fusion.15
  280.0 21.2 %psum.44 = f32[512]{0:T(512)S(1)} all-reduce(f32[512]{0:T(512)S(1)} %fusion.15), channel_id=1, replica_groups=mesh['beam'=8,'mp'=4] {'beam'}, use_global_device_ids=true, to_apply=%region_5.0 | all-reduce | flops 512 | bytes 4096 | tf_op jit(solution)/shard_map/psum | solution.py:107
  301.2 1.3 broadcast_multiply_fusion
  302.5 0.2 copy.41
  302.7 0.1 subtract_convert_fusion.1
  302.9 0.1 copy.42
  303.0 2.5 multiply_bitcast_fusion
  305.6 0.9 copy.55
  306.5 1.4 subtract_convert_fusion
  307.9 1.2 pad_maximum_fusion
  309.0 0.5 copy.64
  309.6 0.7 convolution_convert_fusion
  310.4 0.2 copy.57
  310.6 0.5 fusion.43
  311.1 0.1 copy.54
  311.2 22.1 %multiply_reduce_fusion = (f32[192,2,8]{2,1,0:T(2,128)S(1)}, f32[192,2,8,512]{3,2,1,0:T(8,128)}) fusion(bf16[192,2,8,128]{3,2,1,0:T(8,128)(2,1)S(1)} %bitcast.66, bf16[192,512,2,128]{3,1,2,0:T(8,128)(2,1)} %gather_fusion), kind=kOutput, calls=%fused_computation.8 | convolution fusion | flops 405795840 | bytes 57421824 | tf_op jit(solution)/shard_map/bkgd,blkd->bkgl/dot_general | solution.py:53
  333.4 0.1 copy.45
  333.5 0.2 copy.46
  333.7 3.8 fusion.4
  337.6 0.1 copy.48
  337.8 0.2 copy.51
  337.9 0.1 reshape.154
  338.0 20.1 %add_convert_fusion.1 = bf16[192,2,8,128]{3,2,1,0:T(8,128)(2,1)S(1)} fusion(bf16[192,512,2,128]{3,1,2,0:T(8,128)(2,1)} %gather_fusion.1, f32[192,2,8,512]{3,2,1,0:T(8,128)} %get-tuple-element.19, f32[192,2,8]{2,1,0:T(2,128)S(1)} %copy.48, f32[192,2,8]{2,1,0:T(2,128)S(1)} %copy.46, f32[192,2,128]{2,1,0:T(2,128)S(1)} %reshape.154, f32[192,2,8]{2,1,0:T(2,128)S(1)} %copy.51), kind=kOutput, calls=%fused_computation.30 | convolution fusion | flops 410124288 | bytes 57643008 | tf_op jit(solution)/shard_map/bkgl,blkd->bkgd/dot_general | solution.py:66
  358.1 2.0 convolution_convert_fusion.1
  360.3 99.5 %all-reduce.8.cloned.1.call-done = bf16[512,2048]{1,0:T(8,128)(2,1)} async-done(((bf16[512,2048]{1,0:T(8,128)(2,1)}), bf16[512,2048]{1,0:T(8,128)(2,1)}) %all-reduce.8.cloned.1.call-update) | async-done | bytes 2097168 | tf_op jit(solution)/shard_map/psum | solution.py:178
  459.7 6.5 %fusion.44 = f32[512,1024]{1,0:T(8,128)} fusion(bf16[512,2048]{1,0:T(8,128)(2,1)} %all-reduce.8.cloned.1.call-done, bf16[2048,1024]{1,0:T(8,128)(2,1)} %param.17), kind=kOutput, calls=%fused_computation.81 | convolution fusion | flops 2147483648 | bytes 8388608 | tf_op jit(solution)/shard_map/dot_general | solution.py:182
  466.3 0.6 constant_dynamic-slice_fusion.1
  466.9 0.6 constant_dynamic-slice_fusion
  467.5 29.4 %reduce-scatter.2.cloned.1.call-done = f32[128,1024]{1,0:T(8,128)} async-done(((f32[512,1024]{1,0:T(8,128)}), f32[128,1024]{1,0:T(8,128)}) %reduce-scatter.2.cloned.1.call-update) | async-done | bytes 524304 | tf_op jit(solution)/shard_map/reduce_scatter | solution.py:181
  496.9 1.8 convert_element_type.111
  (44 shorter events, 1.1 us)
Async XLA Ops:
  7.2 98.3 %copy-start = (bf16[1024,256]{1,0:T(8,128)(2,1)S(1)}, bf16[1024,256]{1,0:T(8,128)(2,1)}, u32[]{:S(2)}) copy-start(bf16[1024,256]{1,0:T(8,128)(2,1)} %param.16) | copy-start | bytes 1572868
  7.2 91.4 %all-reduce.6.cloned.1.call-start = ((), (), s32[]{:S(2)}) async-start(), calls=%async_computation.1 | async-start | bytes 2097152 | tf_op jit(solution)/shard_map/psum | solution.py:98
  23.2 40.8 %copy-start.4 = (bf16[1024]{0:T(1024)(128)(2,1)S(1)}, bf16[1024]{0:T(1024)(128)(2,1)}, u32[]{:S(2)}) copy-start(bf16[1024]{0:T(1024)(128)(2,1)} %param.13) | copy-start | bytes 6148
  63.9 237.3 %all-reduce.10.cloned.1.call-start = ((), (), s32[]{:S(2)}) async-start(), calls=%async_computation.4 | async-start | bytes 10485760 | tf_op jit(solution)/shard_map/psum | solution.py:107
  64.0 42.7 %copy-start.5 = (bf16[1024,256]{1,0:T(8,128)(2,1)S(1)}, bf16[1024,256]{1,0:T(8,128)(2,1)}, u32[]{:S(2)}) copy-start(bf16[1024,256]{1,0:T(8,128)(2,1)} %param.15) | copy-start | bytes 1572868
  98.6 6.9 %copy-start.2 = (bf16[512,1024]{1,0:T(8,128)(2,1)S(1)}, bf16[512,1024]{1,0:T(8,128)(2,1)}, u32[]{:S(2)}) copy-start(bf16[512,1024]{1,0:T(8,128)(2,1)} %all-reduce.6.cloned.1.call-done) | copy-start | bytes 3145732
  106.7 1.4 copy-start.3
  108.0 351.7 %all-reduce.8.cloned.1.call-start = ((), (), s32[]{:S(2)}) async-start(), calls=%async_computation.2 | async-start | bytes 4194304 | tf_op jit(solution)/shard_map/psum | solution.py:178
  360.2 136.7 %reduce-scatter.2.cloned.1.call-start = ((), (), s32[]{:S(2)}) async-start(), calls=%async_computation.3 | async-start | bytes 2621440 | tf_op jit(solution)/shard_map/reduce_scatter | solution.py:181
  459.7 38.9 %copy-start.1 = (bf16[1024,256]{1,0:T(8,128)(2,1)S(1)}, bf16[1024,256]{1,0:T(8,128)(2,1)}, u32[]{:S(2)}) copy-start(bf16[1024,256]{1,0:T(8,128)(2,1)} %param.16) | copy-start | bytes 1572868
Sparse Core Ops, SparseCore 0:
  64.0 34.4 all-reduce.5
  108.1 184.6 all-reduce.9
  360.3 99.3 all-reduce.7
  466.4 30.4 reduce-scatter.1
where the time goes:
time: 508 us; the launch traced here: 505 us
  waiting for transfers between devices  163 us (32%)
  local copies, waits for them, and re-layouts  145 us (29%)
  matrix products  102 us (20%)
  blocking collectives  66.2 us (13%)
  between operations  14.7 us (3%)
  other arithmetic  13.1 us (3%)
    psum x1, waiting for transfers between devices, body(): lax.psum(positioned_rows.reshape(BEAMS * REQS, query_width).astype(jnp.bf...  99.5 us
    unnamed x21, local copies, waits for them, and re-layouts  49 us
    dot_general x1, matrix products, body(): looked_up = jnp.dot(one_hot, embedding, preferred_element_type=jnp.float32)  40.7 us
    psum x1, waiting for transfers between devices, body(): embedded = lax.psum(looked_up.astype(jnp.bfloat16), 'mp')  34.6 us
    all_gather x1, blocking collectives, body(): lax.all_gather(parents, 'beam', axis=0, tiled=True)  31.9 us
    reduce_scatter x1, waiting for transfers between devices, body(): lax.psum_scatter(jnp.dot(attended, output_weight, preferred_element_type=...  29.4 us
    gather x1, local copies, waits for them, and re-layouts, body(): slot_keys[slot_index]  25.1 us
    gather x1, local copies, waits for them, and re-layouts, body(): slot_values[slot_index]  23.7 us
  transfers between devices with their start and end apart: 4, of which 3 were waited for; matrix products, arithmetic and copies ran while one was open for 28% of the time, Pallas kernels for 0%

commit v1 on v0

--- a/solution.py
+++ b/solution.py
@@ -175,8 +175,11 @@
         request_start,
         1,
     )
-    attended = lax.psum(
-        positioned_rows.reshape(BEAMS * REQS, query_width).astype(jnp.bfloat16), "beam"
+    attended = jnp.sum(
+        lax.all_gather(
+            positioned_rows.reshape(BEAMS * REQS, query_width).astype(jnp.bfloat16), "beam"
+        ),
+        axis=0,
     )
     attention_out = lax.psum_scatter(
         jnp.dot(attended, output_weight, preferred_element_type=jnp.float32),

time: 508 us -> 641 us (1.26)
  waiting for transfers between devices: 163 us -> 287 us
  other arithmetic: 13.1 us -> 22.6 us
    all_gather x0 -> x1, waiting for transfers between devices: none -> 224 us  [body(): lax.all_gather(positioned_rows.reshape(BEAMS * REQS, query_width).astype(...]
    psum x1 -> x0, waiting for transfers between devices: 99.5 us -> none  [body(): lax.psum(positioned_rows.reshape(BEAMS * REQS, query_width).astype(jnp.bf...]
    reduce_sum x0 -> x1, other arithmetic: none -> 9.45 us  [body(): jnp.sum(lax.all_gather(positioned_rows.reshape(BEAMS * REQS, query_width)...]
  transfers between devices with their start and end apart: 4 -> 4, of which waited for: 3 -> 3; matrix products, arithmetic and copies ran while one was open for 28% -> 22% of each run, Pallas kernels for 0% -> 0%
where the time goes in v1:
time: 641 us; the launch traced here: 638 us
  waiting for transfers between devices  287 us (45%)
  local copies, waits for them, and re-layouts  145 us (23%)
  matrix products  102 us (16%)
  blocking collectives  66.2 us (10%)
  other arithmetic  22.6 us (4%)
  between operations  14.7 us (2%)
    all_gather x1, waiting for transfers between devices, body(): lax.all_gather(positioned_rows.reshape(BEAMS * REQS, query_width).astype(...  224 us
    unnamed x21, local copies, waits for them, and re-layouts  49 us
    dot_general x1, matrix products, body(): looked_up = jnp.dot(one_hot, embedding, preferred_element_type=jnp.float32)  40.7 us
    psum x1, waiting for transfers between devices, body(): embedded = lax.psum(looked_up.astype(jnp.bfloat16), 'mp')  34.6 us
    all_gather x1, blocking collectives, body(): lax.all_gather(parents, 'beam', axis=0, tiled=True)  31.9 us
    reduce_scatter x1, waiting for transfers between devices, body(): lax.psum_scatter(jnp.dot(attended, output_weight, preferred_element_type=...  28.2 us
    gather x1, local copies, waits for them, and re-layouts, body(): slot_keys[slot_index]  25.1 us
    gather x1, local copies, waits for them, and re-layouts, body(): slot_values[slot_index]  23.7 us
  transfers between devices with their start and end apart: 4, of which 3 were waited for; matrix products, arithmetic and copies ran while one was open for 22% of the time, Pallas kernels for 0%

profile of v1, /device:TPU:0, one launch (start us, length us, event | category | flops | bytes accessed | tf_op | source)
XLA Modules:
  0.0 638.0 jit_solution(7929236506106682877)
XLA Ops:
  7.3 1.3 dynamic-slice
  9.2 0.9 dynamic-update-slice
  10.1 13.1 %all-reduce = s32[512]{0:T(512)S(1)} all-reduce(s32[512]{0:T(512)S(1)} %dynamic-update-slice), channel_id=1, replica_groups=mesh['beam'=8,'mp'=4] {'beam'}, use_global_device_ids=true, to_apply=%add | all-reduce | flops 512 | bytes 4096
  23.2 40.7 %fusion.16 = bf16[512,1024]{1,0:T(8,128)(2,1)} fusion(bf16[32064,1024]{1,0:T(8,128)(2,1)} %param.12, s32[32064]{0:T(1024)S(1)} %iota_add_fusion, s32[512]{0:T(512)S(1)} %all-reduce), kind=kOutput, calls=%fused_computation.31 | convolution fusion | flops 33638481920 | bytes 66845952 | tf_op jit(solution)/shard_map/dot_general | solution.py:97
  64.0 34.6 %all-reduce.5.cloned.1.call-done = bf16[512,1024]{1,0:T(8,128)(2,1)} async-done(((bf16[512,1024]{1,0:T(8,128)(2,1)}), bf16[512,1024]{1,0:T(8,128)(2,1)}) %all-reduce.5.cloned.1.call-update) | async-done | bytes 1048592 | tf_op jit(solution)/shard_map/psum | solution.py:98
  98.6 6.9 %fusion.23 = f32[512,2048]{1,0:T(8,128)} fusion(bf16[1024,2048]{1,0:T(8,128)(2,1)} %param.14, bf16[512,1024]{1,0:T(8,128)(2,1)} %all-reduce.5.cloned.1.call-done, f32[1024]{0:T(1024)S(1)} %convert_element_type.100), kind=kOutput, calls=%fused_computation.34 | convolution fusion | flops 2149056512 | bytes 9441280 | tf_op jit(solution)/shard_map/dot_general | solution.py:102
  105.5 1.2 fusion.19
  106.7 1.3 fusion.21
  108.1 31.9 %all_gather.12 = s32[64,8,1]{1,2,0:T(1,128)S(1)} all-gather(s32[8,8,1]{1,2,0:T(1,128)S(1)} %copy-done.3), channel_id=1, replica_groups=mesh['beam'=8,'mp'=4] {'beam'}, dimensions={0}, use_global_device_ids=true | all-gather | bytes 2304 | tf_op jit(solution)/shard_map/all_gather | solution.py:90
  140.1 0.3 reduce-window.9
  140.7 22.5 %copy.43 = bf16[64,512,256]{1,2,0:T(8,128)(2,1)} copy(bf16[64,512,256]{2,1,0:T(8,128)(2,1)} %param.18) | data formatting | bytes 33554432 | tf_op args[8]
  163.2 22.2 %copy.44 = bf16[64,512,2,128]{3,1,2,0:T(8,128)(2,1)} copy(bf16[64,512,2,128]{1,3,2,0:T(8,128)(2,1)} %bitcast.62) | data formatting | bytes 33554432 | tf_op jit(solution)/shard_map/reshape | solution.py:133
  185.4 22.5 %copy.49 = bf16[64,512,256]{1,2,0:T(8,128)(2,1)} copy(bf16[64,512,256]{2,1,0:T(8,128)(2,1)} %param.19) | data formatting | bytes 33554432 | tf_op args[9]
  208.0 22.4 %copy.50 = bf16[64,512,2,128]{3,1,2,0:T(8,128)(2,1)} copy(bf16[64,512,2,128]{1,3,2,0:T(8,128)(2,1)} %bitcast.63) | data formatting | bytes 33554432 | tf_op jit(solution)/shard_map/reshape | solution.py:134
  230.4 0.1 slice_reduce_fusion
  230.6 0.2 select_reduce_fusion
  230.8 25.1 %gather_fusion = bf16[192,512,2,128]{3,1,2,0:T(8,128)(2,1)} fusion(bf16[64,512,2,128]{3,1,2,0:T(8,128)(2,1)} %copy.44, s32[1024]{0:T(1024)S(1)} %pad_clamp_fusion), kind=kCustom, calls=%fused_computation | custom fusion | bytes 100664064 | tf_op jit(solution)/shard_map/gather | solution.py:160
  255.9 23.7 %gather_fusion.1 = bf16[192,512,2,128]{3,1,2,0:T(8,128)(2,1)} fusion(bf16[64,512,2,128]{3,1,2,0:T(8,128)(2,1)} %copy.50, s32[1024]{0:T(1024)S(1)} %pad_clamp_fusion), kind=kCustom, calls=%fused_computation.1 | custom fusion | bytes 100664064 | tf_op jit(solution)/shard_map/gather | solution.py:161
  279.7 0.3 fusion.15
  280.0 21.2 %psum.37 = f32[512]{0:T(512)S(1)} all-reduce(f32[512]{0:T(512)S(1)} %fusion.15), channel_id=1, replica_groups=mesh['beam'=8,'mp'=4] {'beam'}, use_global_device_ids=true, to_apply=%region_5.0 | all-reduce | flops 512 | bytes 4096 | tf_op jit(solution)/shard_map/psum | solution.py:107
  301.2 1.3 broadcast_multiply_fusion
  302.5 0.2 copy.41
  302.7 0.1 subtract_convert_fusion.1
  302.9 0.1 copy.42
  303.0 2.5 multiply_bitcast_fusion
  305.6 0.9 copy.55
  306.5 1.4 subtract_convert_fusion
  307.9 1.2 pad_maximum_fusion
  309.0 0.5 copy.64
  309.6 0.7 convolution_convert_fusion
  310.4 0.2 copy.57
  310.6 0.5 fusion.43
  311.1 0.1 copy.54
  311.2 22.1 %multiply_reduce_fusion = (f32[192,2,8]{2,1,0:T(2,128)S(1)}, f32[192,2,8,512]{3,2,1,0:T(8,128)}) fusion(bf16[192,2,8,128]{3,2,1,0:T(8,128)(2,1)S(1)} %bitcast.68, bf16[192,512,2,128]{3,1,2,0:T(8,128)(2,1)} %gather_fusion), kind=kOutput, calls=%fused_computation.8 | convolution fusion | flops 405795840 | bytes 57421824 | tf_op jit(solution)/shard_map/bkgd,blkd->bkgl/dot_general | solution.py:53
  333.5 0.2 copy.46
  333.7 3.8 fusion.4
  337.6 0.1 copy.48
  337.8 0.2 copy.51
  337.9 0.1 reshape.154
  338.0 20.1 %add_convert_fusion.1 = bf16[192,2,8,128]{3,2,1,0:T(8,128)(2,1)S(1)} fusion(bf16[192,512,2,128]{3,1,2,0:T(8,128)(2,1)} %gather_fusion.1, f32[192,2,8,512]{3,2,1,0:T(8,128)} %get-tuple-element.19, f32[192,2,8]{2,1,0:T(2,128)S(1)} %copy.48, f32[192,2,8]{2,1,0:T(2,128)S(1)} %copy.46, f32[192,2,128]{2,1,0:T(2,128)S(1)} %reshape.154, f32[192,2,8]{2,1,0:T(2,128)S(1)} %copy.51), kind=kOutput, calls=%fused_computation.30 | convolution fusion | flops 410124288 | bytes 57643008 | tf_op jit(solution)/shard_map/bkgl,blkd->bkgd/dot_general | solution.py:66
  358.1 2.1 convolution_convert_fusion.1
  360.3 224.5 %all-gather.3.cloned.1.call-done = bf16[4096,2048]{1,0:T(8,128)(2,1)} async-done(((bf16[512,2048]{1,0:T(8,128)(2,1)}), bf16[4096,2048]{1,0:T(8,128)(2,1)}) %all-gather.3.cloned.1.call-update) | async-done | bytes 16777232 | tf_op jit(solution)/shard_map/all_gather | solution.py:179
  584.8 9.5 %reduce_sum.45 = bf16[512,2048]{1,0:T(8,128)(2,1)S(1)} reduce(bf16[8,512,2048]{2,1,0:T(8,128)(2,1)} %bitcast.65, bf16[]{:T(256)} %constant.80.clone.1), dimensions={0}, to_apply=%region_11.12 | reduce | flops 7340032 | bytes 18874370 | tf_op jit(solution)/shard_map/reduce_sum | solution.py:178
  594.2 5.9 fusion.44
  600.2 0.6 constant_dynamic-slice_fusion.1
  600.8 0.6 constant_dynamic-slice_fusion
  601.4 28.2 %reduce-scatter.2.cloned.1.call-done = f32[128,1024]{1,0:T(8,128)} async-done(((f32[512,1024]{1,0:T(8,128)}), f32[128,1024]{1,0:T(8,128)}) %reduce-scatter.2.cloned.1.call-update) | async-done | bytes 524304 | tf_op jit(solution)/shard_map/reduce_scatter | solution.py:184
  629.7 1.8 convert_element_type.113
  (45 shorter events, 1.2 us)
Async XLA Ops:
  7.2 98.3 %copy-start = (bf16[1024,256]{1,0:T(8,128)(2,1)S(1)}, bf16[1024,256]{1,0:T(8,128)(2,1)}, u32[]{:S(2)}) copy-start(bf16[1024,256]{1,0:T(8,128)(2,1)} %param.16) | copy-start | bytes 1572868
  7.2 91.4 %all-reduce.5.cloned.1.call-start = ((), (), s32[]{:S(2)}) async-start(), calls=%async_computation.1 | async-start | bytes 2097152 | tf_op jit(solution)/shard_map/psum | solution.py:98
  23.2 40.8 %copy-start.4 = (bf16[1024]{0:T(1024)(128)(2,1)S(1)}, bf16[1024]{0:T(1024)(128)(2,1)}, u32[]{:S(2)}) copy-start(bf16[1024]{0:T(1024)(128)(2,1)} %param.13) | copy-start | bytes 6148
  63.9 237.3 %all-reduce.7.cloned.1.call-start = ((), (), s32[]{:S(2)}) async-start(), calls=%async_computation.4 | async-start | bytes 10485760 | tf_op jit(solution)/shard_map/psum | solution.py:107
  64.0 42.7 %copy-start.5 = (bf16[1024,256]{1,0:T(8,128)(2,1)S(1)}, bf16[1024,256]{1,0:T(8,128)(2,1)}, u32[]{:S(2)}) copy-start(bf16[1024,256]{1,0:T(8,128)(2,1)} %param.15) | copy-start | bytes 1572868
  98.6 6.9 %copy-start.2 = (bf16[512,1024]{1,0:T(8,128)(2,1)S(1)}, bf16[512,1024]{1,0:T(8,128)(2,1)}, u32[]{:S(2)}) copy-start(bf16[512,1024]{1,0:T(8,128)(2,1)} %all-reduce.5.cloned.1.call-done) | copy-start | bytes 3145732
  106.7 1.4 copy-start.3
  108.0 476.8 %all-gather.3.cloned.1.call-start = ((), (), s32[]{:S(2)}) async-start(), calls=%async_computation.3 | async-start | bytes 18874368 | tf_op jit(solution)/shard_map/all_gather | solution.py:179
  360.3 269.4 %reduce-scatter.2.cloned.1.call-start = ((), (), s32[]{:S(2)}) async-start(), calls=%async_computation.2 | async-start | bytes 2621440 | tf_op jit(solution)/shard_map/reduce_scatter | solution.py:184
  594.2 37.2 %copy-start.1 = (bf16[1024,256]{1,0:T(8,128)(2,1)S(1)}, bf16[1024,256]{1,0:T(8,128)(2,1)}, u32[]{:S(2)}) copy-start(bf16[1024,256]{1,0:T(8,128)(2,1)} %param.16) | copy-start | bytes 1572868
Sparse Core Ops, SparseCore 0:
  64.0 34.4 all-reduce.4
  108.1 184.6 all-reduce.6
  360.4 224.3 all-gather.2
  600.3 29.3 reduce-scatter.1
